TPU v7x, 32 devices: a whole 2x2x4 slice. The times are simulated.
32 devices in a mesh: node: 8 (over y, x, core), grp: 4 (over z).
Axes of the slice: x: 2, y: 2, z: 4, core: 2. Of those that a mesh axis runs over, the one named last changes fastest.
Arguments:
- tokens: bfloat16 [12288, 1792], P(('node', 'grp')), may hold values from -6 to 6
- cotangent: bfloat16 [12288, 1792], P(('node', 'grp')), may hold values from -6 to 6
- gate_weight: bfloat16 [1792, 1024], P('node'), may hold values from -0.125 to 0.125
- up_weight: bfloat16 [1792, 1024], P('node'), may hold values from -0.125 to 0.125
- down_weight_t: bfloat16 [1792, 1024], P('node'), may hold values from -0.125 to 0.125
- error_memory: bfloat16 [4, 1792, 3072], P('grp', 'node'), may hold values from -4 to 4
- q_init: float32 [3, 1024, 32], replicated, may hold values from -6 to 6
Outputs:
- token_grad: bfloat16 [12288, 1792], P(('node', 'grp'))
- new_error: bfloat16 [4, 1792, 3072], P('grp', 'node')
- p_hat: float32 [3, 1792, 32], P(None, 'node')
- q_new: float32 [3, 1024, 32], replicated
All inputs are finite; a program needn't handle non-finite values.
Results may differ from a plain program's by a relative error of at most 0.012.
Values may be sent and summed in bfloat16 or wider, within the bound.
A program may use at most 192 MiB of HBM per device.

v0:
```python
import math
import jax
import jax.numpy as jnp
from jax import lax
from jax.sharding import PartitionSpec as P


def gelu_parts(value):
    coeff = math.sqrt(2.0 / math.pi)
    inner = coeff * (value + 0.044715 * value * value * value)
    tanh_value = jnp.tanh(inner)
    activation = 0.5 * value * (1.0 + tanh_value)
    slope = 0.5 * (1.0 + tanh_value) + 0.5 * value * (1.0 - tanh_value * tanh_value) * coeff * (
        1.0 + 3.0 * 0.044715 * value * value
    )
    return (activation, slope)


def contract_rows(left_side, right_side):
    return lax.dot_general(
        left_side, right_side, (((0,), (0,)), ((), ())), preferred_element_type=jnp.float32
    )


def on_device(tokens, cotangent, gate_weight, up_weight, down_weight_t, error_memory, q_init):
    node_count = lax.axis_size("node")
    group_count = lax.axis_size("grp")
    hidden_units = gate_weight.shape[1]
    highest = lax.Precision.HIGHEST
    full_gate, full_up, full_down = (
        lax.all_gather(gate_weight, "node", axis=0, tiled=True),
        lax.all_gather(up_weight, "node", axis=0, tiled=True),
        lax.all_gather(down_weight_t, "node", axis=0, tiled=True),
    )
    gate_pre = jnp.dot(tokens, full_gate, preferred_element_type=jnp.float32)
    up_pre = jnp.dot(tokens, full_up, preferred_element_type=jnp.float32)
    activation, slope = gelu_parts(gate_pre)
    hidden = (activation * up_pre).astype(jnp.bfloat16)
    back_hidden = jnp.dot(cotangent, full_down, preferred_element_type=jnp.float32)
    grad_up = (back_hidden * activation).astype(jnp.bfloat16)
    grad_gate = (back_hidden * up_pre * slope).astype(jnp.bfloat16)
    token_grad = (
        lax.dot_general(
            grad_gate, full_gate, (((1,), (1,)), ((), ())), preferred_element_type=jnp.float32
        )
        + lax.dot_general(
            grad_up, full_up, (((1,), (1,)), ((), ())), preferred_element_type=jnp.float32
        )
    ).astype(jnp.bfloat16)
    gate_up = jnp.concatenate([grad_gate, grad_up], axis=1)
    token_cols, cot_cols = (
        lax.all_to_all(tokens, "node", split_axis=1, concat_axis=0, tiled=True),
        lax.all_to_all(cotangent, "node", split_axis=1, concat_axis=0, tiled=True),
    )
    piece_gu = lax.all_gather(gate_up, "node", axis=0, tiled=True)
    piece_hidden = lax.all_gather(hidden, "node", axis=0, tiled=True)
    summed = jnp.concatenate(
        [contract_rows(token_cols, piece_gu), contract_rows(cot_cols, piece_hidden)], axis=1
    )
    grad_scale = 1.0 / math.sqrt(tokens.shape[0] * node_count)
    merged = summed * grad_scale + error_memory[0].astype(jnp.float32)
    blocks = [merged[:, m * hidden_units : (m + 1) * hidden_units] for m in range(3)]
    row_terms = jnp.stack([jnp.dot(blocks[m], q_init[m], precision=highest) for m in range(3)])
    power_rows = lax.psum(row_terms.astype(jnp.bfloat16), "grp").astype(jnp.float32) / group_count
    local_gram = jnp.einsum("mdr,mds->mrs", power_rows, power_rows, precision=highest)
    gram_matrix = lax.psum(local_gram, "node")
    hats = []
    for m in range(3):
        factor = jnp.linalg.cholesky(gram_matrix[m])
        hats.append(jax.scipy.linalg.solve_triangular(factor, power_rows[m].T, lower=True).T)
    col_terms = jnp.stack([jnp.dot(blocks[m].T, hats[m], precision=highest) for m in range(3)])
    q_new = lax.psum(col_terms, ("node", "grp")) / group_count
    errors = [blocks[m] - jnp.dot(hats[m], q_new[m].T, precision=highest) for m in range(3)]
    new_error = jnp.concatenate(errors, axis=1).astype(jnp.bfloat16)[None]
    return (token_grad, new_error, jnp.stack(hats), q_new)


def solution(mesh):
    return jax.shard_map(
        on_device,
        mesh=mesh,
        in_specs=(
            P(("node", "grp"), None),
            P(("node", "grp"), None),
            P("node", None),
            P("node", None),
            P("node", None),
            P("grp", "node", None),
            P(),
        ),
        out_specs=(P(("node", "grp"), None), P("grp", "node", None), P(None, "node", None), P()),
        check_vma=False,
    )
```

profile of v0, /device:TPU:0, one launch (start us, length us, event | category | flops | bytes accessed | tf_op | source)
XLA Modules:
  0.0 512.1 jit_solution(15546751805123783097)
XLA Ops:
  9.4 37.6 %all-gather.6.cloned.1.call-done = bf16[1792,1024]{1,0:T(8,128)(2,1)} async-done(((bf16[224,1024]{1,0:T(8,128)(2,1)}), bf16[1792,1024]{1,0:T(8,128)(2,1)}) %all-gather.6.cloned.1.call-update) | async-done | bytes 3670032 | tf_op jit(solution)/shard_map/all_gather | solution.py:33
  47.0 5.2 %fusion.44 = f32[384,1024]{1,0:T(8,128)} fusion(bf16[384,1792]{1,0:T(8,128)(2,1)} %param.11, bf16[1792,1024]{1,0:T(8,128)(2,1)} %all-gather.6.cloned.1.call-done), kind=kOutput, calls=%fused_computation.92 | convolution fusion | flops 1409286144 | bytes 6619136 | tf_op jit(solution)/shard_map/dot_general | solution.py:39
  52.2 31.1 %all-gather.10.cloned.1.call-done = bf16[1792,1024]{1,0:T(8,128)(2,1)} async-done(((bf16[224,1024]{1,0:T(8,128)(2,1)}), bf16[1792,1024]{1,0:T(8,128)(2,1)}) %all-gather.10.cloned.1.call-update) | async-done | bytes 3670032 | tf_op jit(solution)/shard_map/all_gather | solution.py:31
  83.3 4.8 fusion.45
  88.1 31.5 %all-gather.8.cloned.1.call-done = bf16[1792,1024]{1,0:T(8,128)(2,1)} async-done(((bf16[224,1024]{1,0:T(8,128)(2,1)}), bf16[1792,1024]{1,0:T(8,128)(2,1)}) %all-gather.8.cloned.1.call-update) | async-done | bytes 3670032 | tf_op jit(solution)/shard_map/all_gather | solution.py:32
  119.6 6.4 %multiply_convert_fusion = (bf16[384,1024]{1,0:T(8,128)(2,1)}, bf16[384,1024]{1,0:T(8,128)(2,1)S(1)}, bf16[384,1024]{1,0:T(8,128)(2,1)S(1)}) fusion(f32[384,1024]{1,0:T(8,128)} %fusion.45, f32[384,1024]{1,0:T(8,128)} %fusion.44, bf16[384,1792]{1,0:T(8,128)(2,1)S(1)} %copy-done.2, bf16[1792,1024]{1,0:T(8,128)(2,1)} %all-gather.8.cloned.1.call-done), kind=kOutput, calls=%fused_computation.15 | convolution fusion | flops 1419116544 | bytes 10551296 | tf_op jit(solution)/shard_map/dot_general | solution.py:36
  129.6 1.5 copy.17
  131.1 3.6 all-to-all-start.1
  134.7 1.5 copy.15
  136.3 24.3 %all-to-all-done.1 = bf16[384,8,224]{0,2,1:T(8,128)(2,1)S(1)} async-done(((bf16[384,8,224]{0,2,1:T(8,128)(2,1)}), bf16[384,8,224]{0,2,1:T(8,128)(2,1)S(1)}, u32[]{:S(2)}, u32[]{:S(2)}) %all-to-all-start.1) | async-done | bytes 1376288 | tf_op jit(solution)/shard_map/all_to_all | solution.py:53
  160.5 3.6 all-to-all-start
  165.7 31.9 %all-to-all-done = bf16[384,8,224]{0,2,1:T(8,128)(2,1)S(1)} async-done(((bf16[384,8,224]{0,2,1:T(8,128)(2,1)}), bf16[384,8,224]{0,2,1:T(8,128)(2,1)S(1)}, u32[]{:S(2)}, u32[]{:S(2)}) %all-to-all-start) | async-done | bytes 1376288 | tf_op jit(solution)/shard_map/all_to_all | solution.py:52
  198.9 5.4 %fusion.46 = f32[384,1792]{1,0:T(8,128)} fusion(bf16[384,1024]{1,0:T(8,128)(2,1)S(1)} %copy-done.8, bf16[1792,1024]{1,0:T(8,128)(2,1)} %all-gather.10.cloned.1.call-done), kind=kOutput, calls=%fused_computation.94 | convolution fusion | flops 1409286144 | bytes 7208960 | tf_op jit(solution)/shard_map/dot_general | solution.py:43
  204.3 5.4 %convolution_bitcast_fusion.1 = f32[224,1024]{1,0:T(8,128)} fusion(bf16[3072,224]{0,1:T(8,128)(2,1)S(1)} %bitcast.133, bf16[3072,1024]{1,0:T(8,128)(2,1)} %all-gather.14.cloned.1.call-done), kind=kOutput, calls=%fused_computation.19 | convolution fusion | flops 1409286144 | bytes 8585216 | tf_op jit(solution)/shard_map/dot_general | solution.py:20
  209.7 64.7 %all-gather.12.cloned.1.call-done = bf16[3072,2048]{1,0:T(8,128)(2,1)} async-done(((bf16[384,2048]{1,0:T(8,128)(2,1)}), bf16[3072,2048]{1,0:T(8,128)(2,1)}) %all-gather.12.cloned.1.call-update) | async-done | bytes 12582928 | tf_op jit(solution)/shard_map/all_gather | solution.py:55
  274.4 6.4 %convolution_bitcast_fusion = f32[224,2048]{1,0:T(8,128)S(1)} fusion(bf16[3072,224]{0,1:T(8,128)(2,1)S(1)} %bitcast.134, bf16[3072,2048]{1,0:T(8,128)(2,1)} %all-gather.12.cloned.1.call-done), kind=kOutput, calls=%fused_computation.4 | convolution fusion | flops 2818572288 | bytes 15794176 | tf_op jit(solution)/shard_map/dot_general | solution.py:20
  285.2 20.5 %psum.21 = bf16[3,224,32]{1,2,0:T(8,128)(2,1)} all-reduce(bf16[3,224,32]{1,2,0:T(8,128)(2,1)} %pad_maximum_fusion.4), channel_id=1, replica_groups=mesh['node'=8,'grp'=4] {'grp'}, use_global_device_ids=true, to_apply=%region_0.0 | all-reduce | flops 21504 | bytes 86016 | tf_op jit(solution)/shard_map/psum | solution.py:64
  305.6 1.7 fusion.33
  307.4 1.4 convert_multiply_fusion
  308.8 24.0 %psum.22 = f32[3,32,32]{1,2,0:T(8,128)} all-reduce(f32[3,32,32]{1,2,0:T(8,128)} %fusion.33), channel_id=1, replica_groups=mesh['node'=8,'grp'=4] {'node'}, use_global_device_ids=true, to_apply=%region_1.0 | all-reduce | flops 3072 | bytes 24576 | tf_op jit(solution)/shard_map/psum | solution.py:66
  339.2 3.6 cholesky.59
  344.8 3.8 custom-call.7
  348.5 3.6 cholesky.70
  354.1 3.2 custom-call.8
  357.3 1.6 fusion.32
  358.9 1.6 fusion.31
  360.5 3.6 cholesky.81
  366.0 3.2 custom-call.9
  370.9 1.4 convolution_bitcast_fusion.3
  373.8 5.7 %fusion = bf16[384,1792]{1,0:T(8,128)(2,1)} fusion(f32[384,1792]{1,0:T(8,128)} %fusion.46, bf16[384,1024]{1,0:T(8,128)(2,1)S(1)} %get-tuple-element.8, bf16[1792,1024]{1,0:T(8,128)(2,1)} %all-gather.8.cloned.1.call-done), kind=kOutput, calls=%fused_computation.1 | convolution fusion | flops 1410662400 | bytes 8585216 | tf_op jit(solution)/shard_map/dot_general | solution.py:46
  380.2 119.2 %all-reduce.2.cloned.1.call-done = f32[3,1024,32]{1,2,0:T(8,128)} async-done(((f32[3,1024,32]{1,2,0:T(8,128)}), f32[3,1024,32]{1,2,0:T(8,128)}) %all-reduce.2.cloned.1.call-update) | async-done | bytes 393232 | tf_op jit(solution)/shard_map/psum | solution.py:72
  500.4 1.8 fusion.12
  (78 shorter events, 33.0 us)
Async XLA Ops:
  7.2 39.8 %all-gather.6.cloned.1.call-start = ((), (), s32[]{:S(2)}) async-start(), calls=%async_computation.2 | async-start | bytes 4128768 | tf_op jit(solution)/shard_map/all_gather | solution.py:33
  7.9 75.4 %all-gather.10.cloned.1.call-start = ((), (), s32[]{:S(2)}) async-start(), calls=%async_computation.4 | async-start | bytes 4128768 | tf_op jit(solution)/shard_map/all_gather | solution.py:31
  8.6 111.0 %all-gather.8.cloned.1.call-start = ((), (), s32[]{:S(2)}) async-start(), calls=%async_computation.3 | async-start | bytes 4128768 | tf_op jit(solution)/shard_map/all_gather | solution.py:32
  9.4 73.9 %copy-start.2 = (bf16[384,1792]{1,0:T(8,128)(2,1)S(1)}, bf16[384,1792]{1,0:T(8,128)(2,1)}, u32[]{:S(2)}) copy-start(bf16[384,1792]{1,0:T(8,128)(2,1)} %param.10) | copy-start | bytes 4128772
  9.4 194.9 %all-gather.14.cloned.1.call-start = ((), (), s32[]{:S(2)}) async-start(), calls=%async_computation.6 | async-start | bytes 7077888 | tf_op jit(solution)/shard_map/all_gather | solution.py:56
  126.0 0.9 copy-start.7
  126.0 148.4 %all-gather.12.cloned.1.call-start = ((), (), s32[]{:S(2)}) async-start(), calls=%async_computation.5 | async-start | bytes 14155776 | tf_op jit(solution)/shard_map/all_gather | solution.py:55
  128.2 1.3 copy-start.1
  131.1 29.4 %all-to-all-start.1 = ((bf16[384,8,224]{0,2,1:T(8,128)(2,1)}), bf16[384,8,224]{0,2,1:T(8,128)(2,1)S(1)}, u32[]{:S(2)}, u32[]{:S(2)}) async-start(bf16[384,8,224]{0,2,1:T(8,128)(2,1)} %bitcast.3), calls=%async_computation.1 | async-start | bytes 2752512 | tf_op jit(solution)/shard_map/all_to_all | solution.py:53
  160.5 37.1 %all-to-all-start = ((bf16[384,8,224]{0,2,1:T(8,128)(2,1)}), bf16[384,8,224]{0,2,1:T(8,128)(2,1)S(1)}, u32[]{:S(2)}, u32[]{:S(2)}) async-start(bf16[384,8,224]{0,2,1:T(8,128)(2,1)} %bitcast), calls=%async_computation | async-start | bytes 2752512 | tf_op jit(solution)/shard_map/all_to_all | solution.py:52
  164.1 335.3 %all-reduce.2.cloned.1.call-start = ((), (), s32[]{:S(2)}) async-start(), calls=%async_computation.7 | async-start | bytes 786432 | tf_op jit(solution)/shard_map/psum | solution.py:72
  197.6 1.3 copy-start.8
  198.9 5.4 %copy-start.4 = (bf16[8,28,8,384]{3,2,0,1:T(8,128)(2,1)S(1)}, bf16[8,28,8,384]{3,2,0,1:T(8,128)(2,1)}, u32[]{:S(2)}) copy-start(bf16[8,28,8,384]{3,2,0,1:T(8,128)(2,1)} %copy.25) | copy-start | bytes 4128772
  204.3 70.1 %copy-start.5 = (bf16[8,28,8,384]{3,2,0,1:T(8,128)(2,1)S(1)}, bf16[8,28,8,384]{3,2,0,1:T(8,128)(2,1)}, u32[]{:S(2)}) copy-start(bf16[8,28,8,384]{3,2,0,1:T(8,128)(2,1)} %copy.24) | copy-start | bytes 4128772
  274.4 6.4 %copy-start.3 = (bf16[1,224,3072]{2,1,0:T(8,128)(2,1)S(1)}, bf16[1,224,3072]{2,1,0:T(8,128)(2,1)}, u32[]{:S(2)}) copy-start(bf16[1,224,3072]{2,1,0:T(8,128)(2,1)} %param.15) | copy-start | bytes 4128772
  274.4 6.4 %copy-start.6 = (f32[224,1024]{1,0:T(8,128)S(1)}, f32[224,1024]{1,0:T(8,128)}, u32[]{:S(2)}) copy-start(f32[224,1024]{1,0:T(8,128)} %convolution_bitcast_fusion.1) | copy-start | bytes 2752516
  280.8 1.0 copy-start.16
  369.2 3.1 copy-start.9
  370.2 2.8 copy-start.14
  373.8 5.7 %copy-start.10 = (f32[32,224]{1,0:T(8,128)S(1)}, f32[32,224]{1,0:T(8,128)}, u32[]{:S(2)}) copy-start(f32[32,224]{1,0:T(8,128)} %fusion.32) | copy-start | bytes 86020
  373.8 5.7 %copy-start.12 = (f32[32,224]{1,0:T(8,128)S(1)}, f32[32,224]{1,0:T(8,128)}, u32[]{:S(2)}) copy-start(f32[32,224]{1,0:T(8,128)} %fusion.31) | copy-start | bytes 86020
  373.8 5.7 %copy-start.15 = (f32[32,224]{1,0:T(8,128)S(1)}, f32[32,224]{1,0:T(8,128)}, u32[]{:S(2)}) copy-start(f32[32,224]{1,0:T(8,128)} %copy-done.14) | copy-start | bytes 86020
  379.5 122.7 %copy-start.13 = (f32[32,224]{1,0:T(8,128)S(1)}, f32[32,224]{1,0:T(8,128)}, u32[]{:S(2)}) copy-start(f32[32,224]{1,0:T(8,128)} %fusion.31) | copy-start | bytes 86020
  500.4 3.7 copy-start
  500.4 2.7 copy-start.11
Sparse Core Ops, SparseCore 0:
  9.9 37.0 all-gather.5
  48.9 34.3 all-gather.9
  85.2 34.3 all-gather.7
  126.1 74.4 all-gather.13
  202.4 71.9 all-gather.11
  373.9 125.4 all-reduce.1
where the time goes:
time: 514 us; the launch traced here: 512 us
  waiting for transfers between devices  342 us (67%)
  matrix products  54.2 us (11%)
  blocking collectives  44.5 us (9%)
  other arithmetic  35.7 us (7%)
  between operations  14.4 us (3%)
  local copies, waits for them, and re-layouts  13.4 us (3%)
  starting transfers between devices  7.6 us (1%)
    psum x1, waiting for transfers between devices, on_device(): q_new = lax.psum(col_terms, ('node', 'grp')) / group_count  119 us
    all_gather x1, waiting for transfers between devices, on_device(): piece_gu = lax.all_gather(gate_up, 'node', axis=0, tiled=True)  64.7 us
    all_gather x1, waiting for transfers between devices, on_device(): lax.all_gather(down_weight_t, 'node', axis=0, tiled=True)  37.6 us
    all_to_all x1, waiting for transfers between devices, on_device(): lax.all_to_all(tokens, 'node', split_axis=1, concat_axis=0, tiled=True)  31.9 us
    all_gather x1, waiting for transfers between devices, on_device(): lax.all_gather(up_weight, 'node', axis=0, tiled=True)  31.5 us
    all_gather x1, waiting for transfers between devices, on_device(): lax.all_gather(gate_weight, 'node', axis=0, tiled=True)  31.1 us
    all_to_all x1, waiting for transfers between devices, on_device(): lax.all_to_all(cotangent, 'node', split_axis=1, concat_axis=0, tiled=True)  24.3 us
    psum x1, blocking collectives, on_device(): gram_matrix = lax.psum(local_gram, 'node')  24 us
  transfers between devices with their start and end apart: 8, of which 7 were waited for; matrix products, arithmetic and copies ran while one was open for 7% of the time, Pallas kernels for 0%

commit v1 on v0

--- a/solution.py
+++ b/solution.py
@@ -49,7 +49,12 @@
     ).astype(jnp.bfloat16)
     gate_up = jnp.concatenate([grad_gate, grad_up], axis=1)
     token_cols, cot_cols = (
-        lax.all_to_all(tokens, "node", split_axis=1, concat_axis=0, tiled=True),
+        jnp.concatenate(
+            lax.all_to_all(
+                jnp.stack(jnp.split(tokens, lax.axis_size("node"), axis=1), axis=0), "node", 0, 0
+            ),
+            axis=0,
+        ),
         lax.all_to_all(cotangent, "node", split_axis=1, concat_axis=0, tiled=True),
     )
     piece_gu = lax.all_gather(gate_up, "node", axis=0, tiled=True)

time: 514 us -> 498 us (0.969)
  waiting for transfers between devices: 342 us -> 329 us
  local copies, waits for them, and re-layouts: 13.4 us -> 22.3 us
  other arithmetic: 35.7 us -> 30.3 us
    all_to_all x1, waiting for transfers between devices: 24.3 us -> 11.1 us  [on_device(): lax.all_to_all(cotangent, 'node', split_axis=1, concat_axis=0, tiled=True)]
    unnamed x36 -> x58, local copies, waits for them, and re-layouts: 5.8 us -> 18.1 us
    all_gather x1, waiting for transfers between devices: 31.1 us -> 37.6 us  [on_device(): lax.all_gather(gate_weight, 'node', axis=0, tiled=True)]
    all_gather x1, waiting for transfers between devices: 37.6 us -> 31.1 us  [on_device(): lax.all_gather(down_weight_t, 'node', axis=0, tiled=True)]
  transfers between devices with their start and end apart: 8 -> 8, of which waited for: 7 -> 7; matrix products, arithmetic and copies ran while one was open for 7% -> 10% of each run, Pallas kernels for 0% -> 0%
where the time goes in v1:
time: 498 us; the launch traced here: 497 us
  waiting for transfers between devices  329 us (66%)
  matrix products  50.8 us (10%)
  blocking collectives  42.3 us (8%)
  other arithmetic  30.3 us (6%)
  local copies, waits for them, and re-layouts  22.3 us (4%)
  between operations  14.5 us (3%)
  starting transfers between devices  7.58 us (2%)
    psum x1, waiting for transfers between devices, on_device(): q_new = lax.psum(col_terms, ('node', 'grp')) / group_count  119 us
    all_gather x1, waiting for transfers between devices, on_device(): piece_gu = lax.all_gather(gate_up, 'node', axis=0, tiled=True)  64.7 us
    all_gather x1, waiting for transfers between devices, on_device(): lax.all_gather(gate_weight, 'node', axis=0, tiled=True)  37.6 us
    all_to_all x1, waiting for transfers between devices, on_device(): lax.all_to_all(jnp.stack(jnp.split(tokens, lax.axis_size('node'), axis=1)...  31.9 us
    all_gather x1, waiting for transfers between devices, on_device(): lax.all_gather(up_weight, 'node', axis=0, tiled=True)  31.5 us
    all_gather x1, waiting for transfers between devices, on_device(): lax.all_gather(down_weight_t, 'node', axis=0, tiled=True)  31.1 us
    psum x1, blocking collectives, on_device(): gram_matrix = lax.psum(local_gram, 'node')  22.9 us
    psum x1, blocking collectives, on_device(): lax.psum(row_terms.astype(jnp.bfloat16), 'grp').astype(jnp.float32)  19.4 us
  transfers between devices with their start and end apart: 8, of which 7 were waited for; matrix products, arithmetic and copies ran while one was open for 10% of the time, Pallas kernels for 0%

profile of v1, /device:TPU:0, one launch (start us, length us, event | category | flops | bytes accessed | tf_op | source)
XLA Modules:
  0.0 497.1 jit_solution(9300958166592846481)
XLA Ops:
  9.4 37.6 %all-gather.10.cloned.1.call-done = bf16[1792,1024]{1,0:T(8,128)(2,1)} async-done(((bf16[224,1024]{1,0:T(8,128)(2,1)}), bf16[1792,1024]{1,0:T(8,128)(2,1)}) %all-gather.10.cloned.1.call-update) | async-done | bytes 3670032 | tf_op jit(solution)/shard_map/all_gather | solution.py:31
  47.0 5.2 %fusion.46 = f32[384,1024]{1,0:T(8,128)} fusion(bf16[384,1792]{1,0:T(8,128)(2,1)} %param.10, bf16[1792,1024]{1,0:T(8,128)(2,1)} %all-gather.10.cloned.1.call-done), kind=kOutput, calls=%fused_computation.101 | convolution fusion | flops 1409286144 | bytes 6619136 | tf_op jit(solution)/shard_map/dot_general | solution.py:35
  52.2 31.1 %all-gather.6.cloned.1.call-done = bf16[1792,1024]{1,0:T(8,128)(2,1)} async-done(((bf16[224,1024]{1,0:T(8,128)(2,1)}), bf16[1792,1024]{1,0:T(8,128)(2,1)}) %all-gather.6.cloned.1.call-update) | async-done | bytes 3670032 | tf_op jit(solution)/shard_map/all_gather | solution.py:33
  83.3 4.8 fusion.45
  88.1 31.5 %all-gather.8.cloned.1.call-done = bf16[1792,1024]{1,0:T(8,128)(2,1)} async-done(((bf16[224,1024]{1,0:T(8,128)(2,1)}), bf16[1792,1024]{1,0:T(8,128)(2,1)}) %all-gather.8.cloned.1.call-update) | async-done | bytes 3670032 | tf_op jit(solution)/shard_map/all_gather | solution.py:32
  119.6 6.7 %multiply_convert_fusion = (bf16[384,1024]{1,0:T(8,128)(2,1)}, bf16[384,1024]{1,0:T(8,128)(2,1)}, bf16[384,1024]{1,0:T(8,128)(2,1)S(1)}) fusion(f32[384,1024]{1,0:T(8,128)} %fusion.46, f32[384,1024]{1,0:T(8,128)} %fusion.45, bf16[384,1792]{1,0:T(8,128)(2,1)S(1)} %copy-done, bf16[1792,1024]{1,0:T(8,128)(2,1)} %all-gather.8.cloned.1.call-done), kind=kOutput, calls=%fused_computation.14 | convolution fusion | flops 1419116544 | bytes 10551296 | tf_op jit(solution)/shard_map/dot_general | solution.py:36
  126.4 2.7 pad_maximum_fusion
  129.1 1.5 copy.44
  130.7 3.6 all-to-all-start.1
  135.6 1.7 copy.51
  137.3 1.7 copy.52
  139.0 1.7 copy.53
  143.6 1.7 copy.54
  149.7 11.1 %all-to-all-done.1 = bf16[384,8,224]{0,2,1:T(8,128)(2,1)S(1)} async-done(((bf16[384,8,224]{0,2,1:T(8,128)(2,1)}), bf16[384,8,224]{0,2,1:T(8,128)(2,1)S(1)}, u32[]{:S(2)}, u32[]{:S(2)}) %all-to-all-start.1) | async-done | bytes 1376288 | tf_op jit(solution)/shard_map/all_to_all | solution.py:58
  160.8 3.6 all-to-all-start
  166.0 31.9 %all-to-all-done = bf16[8,384,224]{1,2,0:T(8,128)(2,1)S(1)} async-done(((bf16[8,384,224]{1,2,0:T(8,128)(2,1)}), bf16[8,384,224]{1,2,0:T(8,128)(2,1)S(1)}, u32[]{:S(2)}, u32[]{:S(2)}) %all-to-all-start) | async-done | bytes 1376288 | tf_op jit(solution)/shard_map/all_to_all | solution.py:53
  199.2 5.4 %fusion.47 = f32[384,1792]{1,0:T(8,128)} fusion(bf16[384,1024]{1,0:T(8,128)(2,1)S(1)} %copy-done.10, bf16[1792,1024]{1,0:T(8,128)(2,1)} %all-gather.10.cloned.1.call-done), kind=kOutput, calls=%fused_computation.102 | convolution fusion | flops 1409286144 | bytes 7208960 | tf_op jit(solution)/shard_map/dot_general | solution.py:43
  204.6 5.4 %convolution_bitcast_fusion = f32[224,1024]{1,0:T(8,128)} fusion(bf16[3072,224]{0,1:T(8,128)(2,1)S(1)} %bitcast.145, bf16[3072,1024]{1,0:T(8,128)(2,1)} %all-gather.14.cloned.1.call-done), kind=kOutput, calls=%fused_computation.18 | convolution fusion | flops 1409286144 | bytes 8585216 | tf_op jit(solution)/shard_map/dot_general | solution.py:20
  210.0 64.7 %all-gather.12.cloned.1.call-done = bf16[3072,2048]{1,0:T(8,128)(2,1)} async-done(((bf16[384,2048]{1,0:T(8,128)(2,1)}), bf16[3072,2048]{1,0:T(8,128)(2,1)}) %all-gather.12.cloned.1.call-update) | async-done | bytes 12582928 | tf_op jit(solution)/shard_map/all_gather | solution.py:60
  274.8 6.4 %fusion.48 = f32[224,2048]{1,0:T(8,128)S(1)} fusion(bf16[3072,224]{0,1:T(8,128)(2,1)S(1)} %bitcast.146, bf16[3072,2048]{1,0:T(8,128)(2,1)} %all-gather.12.cloned.1.call-done), kind=kOutput, calls=%fused_computation.103 | convolution fusion | flops 2818572288 | bytes 15794176 | tf_op jit(solution)/shard_map/dot_general | solution.py:20
  284.9 19.4 %psum.21 = bf16[3,224,32]{1,2,0:T(8,128)(2,1)S(1)} all-reduce(bf16[3,224,32]{1,2,0:T(8,128)(2,1)S(1)} %pad_maximum_fusion.4), channel_id=1, replica_groups=mesh['node'=8,'grp'=4] {'grp'}, use_global_device_ids=true, to_apply=%region_0.0 | all-reduce | flops 21504 | bytes 86016 | tf_op jit(solution)/shard_map/psum | solution.py:69
  304.5 22.9 %psum.22 = f32[3,32,32]{1,2,0:T(8,128)S(1)} all-reduce(f32[3,32,32]{1,2,0:T(8,128)S(1)} %fusion.33), channel_id=1, replica_groups=mesh['node'=8,'grp'=4] {'node'}, use_global_device_ids=true, to_apply=%region_1.0 | all-reduce | flops 3072 | bytes 24576 | tf_op jit(solution)/shard_map/psum | solution.py:71
  328.3 2.9 cholesky.81
  332.6 2.4 custom-call.9
  337.2 2.9 cholesky.70
  341.4 2.4 custom-call.8
  346.1 3.6 cholesky.59
  351.5 3.2 custom-call.7
  357.0 1.7 pad_maximum_fusion.2
  358.8 5.7 %fusion = bf16[384,1792]{1,0:T(8,128)(2,1)} fusion(f32[384,1792]{1,0:T(8,128)} %fusion.47, bf16[384,1024]{1,0:T(8,128)(2,1)S(1)} %copy-done.9, bf16[1792,1024]{1,0:T(8,128)(2,1)} %all-gather.8.cloned.1.call-done), kind=kOutput, calls=%fused_computation.1 | convolution fusion | flops 1410662400 | bytes 8585216 | tf_op jit(solution)/shard_map/dot_general | solution.py:46
  365.1 119.2 %all-reduce.2.cloned.1.call-done = f32[3,1024,32]{1,2,0:T(8,128)} async-done(((f32[3,1024,32]{1,2,0:T(8,128)}), f32[3,1024,32]{1,2,0:T(8,128)}) %all-reduce.2.cloned.1.call-update) | async-done | bytes 393232 | tf_op jit(solution)/shard_map/psum | solution.py:77
  485.4 1.8 fusion.12
  (102 shorter events, 34.3 us)
Async XLA Ops:
  7.2 39.8 %all-gather.10.cloned.1.call-start = ((), (), s32[]{:S(2)}) async-start(), calls=%async_computation.4 | async-start | bytes 4128768 | tf_op jit(solution)/shard_map/all_gather | solution.py:31
  7.9 75.4 %all-gather.6.cloned.1.call-start = ((), (), s32[]{:S(2)}) async-start(), calls=%async_computation.2 | async-start | bytes 4128768 | tf_op jit(solution)/shard_map/all_gather | solution.py:33
  8.6 111.0 %all-gather.8.cloned.1.call-start = ((), (), s32[]{:S(2)}) async-start(), calls=%async_computation.3 | async-start | bytes 4128768 | tf_op jit(solution)/shard_map/all_gather | solution.py:32
  9.4 73.9 %copy-start.3 = (bf16[384,1792]{1,0:T(8,128)(2,1)S(1)}, bf16[384,1792]{1,0:T(8,128)(2,1)}, u32[]{:S(2)}) copy-start(bf16[384,1792]{1,0:T(8,128)(2,1)} %param.11) | copy-start | bytes 4128772
  9.4 195.2 %all-gather.14.cloned.1.call-start = ((), (), s32[]{:S(2)}) async-start(), calls=%async_computation.6 | async-start | bytes 7077888 | tf_op jit(solution)/shard_map/all_gather | solution.py:61
  52.2 67.4 %copy-start = (bf16[384,1792]{1,0:T(8,128)(2,1)S(1)}, bf16[384,1792]{1,0:T(8,128)(2,1)}, u32[]{:S(2)}) copy-start(bf16[384,1792]{1,0:T(8,128)(2,1)} %param.10) | copy-start | bytes 4128772
  126.3 2.8 copy-start.8
  126.3 148.4 %all-gather.12.cloned.1.call-start = ((), (), s32[]{:S(2)}) async-start(), calls=%async_computation.5 | async-start | bytes 14155776 | tf_op jit(solution)/shard_map/all_gather | solution.py:60
  130.7 30.2 %all-to-all-start.1 = ((bf16[384,8,224]{0,2,1:T(8,128)(2,1)}), bf16[384,8,224]{0,2,1:T(8,128)(2,1)S(1)}, u32[]{:S(2)}, u32[]{:S(2)}) async-start(bf16[384,8,224]{0,2,1:T(8,128)(2,1)} %bitcast.8), calls=%async_computation.1 | async-start | bytes 2752512 | tf_op jit(solution)/shard_map/all_to_all | solution.py:58
  148.6 1.1 copy-start.1
  160.8 37.1 %all-to-all-start = ((bf16[8,384,224]{1,2,0:T(8,128)(2,1)}), bf16[8,384,224]{1,2,0:T(8,128)(2,1)S(1)}, u32[]{:S(2)}, u32[]{:S(2)}) async-start(bf16[8,384,224]{1,2,0:T(8,128)(2,1)} %copy-done.1), calls=%async_computation | async-start | bytes 2752512 | tf_op jit(solution)/shard_map/all_to_all | solution.py:53
  164.4 319.9 %all-reduce.2.cloned.1.call-start = ((), (), s32[]{:S(2)}) async-start(), calls=%async_computation.7 | async-start | bytes 786432 | tf_op jit(solution)/shard_map/psum | solution.py:77
  166.0 33.2 %copy-start.10 = (bf16[384,1024]{1,0:T(8,128)(2,1)S(1)}, bf16[384,1024]{1,0:T(8,128)(2,1)}, u32[]{:S(2)}) copy-start(bf16[384,1024]{1,0:T(8,128)(2,1)} %get-tuple-element.7) | copy-start | bytes 2359300
  199.2 5.4 %copy-start.5 = (bf16[8,28,8,384]{3,2,0,1:T(8,128)(2,1)S(1)}, bf16[8,28,8,384]{3,2,0,1:T(8,128)(2,1)}, u32[]{:S(2)}) copy-start(bf16[8,28,8,384]{3,2,0,1:T(8,128)(2,1)} %copy.60) | copy-start | bytes 4128772
  204.6 70.1 %copy-start.6 = (bf16[8,28,8,384]{3,2,0,1:T(8,128)(2,1)S(1)}, bf16[8,28,8,384]{3,2,0,1:T(8,128)(2,1)}, u32[]{:S(2)}) copy-start(bf16[8,28,8,384]{3,2,0,1:T(8,128)(2,1)} %copy.59) | copy-start | bytes 4128772
  274.8 6.4 %copy-start.4 = (bf16[1,224,3072]{2,1,0:T(8,128)(2,1)S(1)}, bf16[1,224,3072]{2,1,0:T(8,128)(2,1)}, u32[]{:S(2)}) copy-start(bf16[1,224,3072]{2,1,0:T(8,128)(2,1)} %param.15) | copy-start | bytes 4128772
  274.8 6.4 %copy-start.7 = (f32[224,1024]{1,0:T(8,128)S(1)}, f32[224,1024]{1,0:T(8,128)}, u32[]{:S(2)}) copy-start(f32[224,1024]{1,0:T(8,128)} %convolution_bitcast_fusion) | copy-start | bytes 2752516
  281.1 1.0 copy-start.20
  304.3 39.6 %copy-start.19 = (f32[3,224,32]{1,2,0:T(8,128)}, f32[3,224,32]{1,2,0:T(8,128)S(1)}, u32[]{:S(2)}) copy-start(f32[3,224,32]{1,2,0:T(8,128)S(1)} %convert_multiply_fusion) | copy-start | bytes 258052
  335.3 0.6 copy-start.11
  344.1 0.6 copy-start.13
  344.8 14.0 %copy-start.9 = (bf16[384,1024]{1,0:T(8,128)(2,1)S(1)}, bf16[384,1024]{1,0:T(8,128)(2,1)}, u32[]{:S(2)}) copy-start(bf16[384,1024]{1,0:T(8,128)(2,1)} %copy-done.8) | copy-start | bytes 2359300
  355.7 0.6 copy-start.16
  358.8 5.7 %copy-start.12 = (f32[32,224]{1,0:T(8,128)S(1)}, f32[32,224]{1,0:T(8,128)}, u32[]{:S(2)}) copy-start(f32[32,224]{1,0:T(8,128)} %copy-done.11) | copy-start | bytes 86020
  358.8 5.7 %copy-start.14 = (f32[32,224]{1,0:T(8,128)S(1)}, f32[32,224]{1,0:T(8,128)}, u32[]{:S(2)}) copy-start(f32[32,224]{1,0:T(8,128)} %copy-done.13) | copy-start | bytes 86020
  358.8 5.7 %copy-start.17 = (f32[32,224]{1,0:T(8,128)S(1)}, f32[32,224]{1,0:T(8,128)}, u32[]{:S(2)}) copy-start(f32[32,224]{1,0:T(8,128)} %copy-done.16) | copy-start | bytes 86020
  364.5 122.7 %copy-start.15 = (f32[32,224]{1,0:T(8,128)S(1)}, f32[32,224]{1,0:T(8,128)}, u32[]{:S(2)}) copy-start(f32[32,224]{1,0:T(8,128)} %copy-done.13) | copy-start | bytes 86020
  485.4 3.7 copy-start.2
  485.4 2.7 copy-start.18
Sparse Core Ops, SparseCore 0:
  9.9 37.0 all-gather.9
  48.9 34.3 all-gather.5
  85.2 34.3 all-gather.7
  126.5 74.4 all-gather.13
  202.7 71.9 all-gather.11
  358.9 125.3 all-reduce.1
